TPU v7x, 32 devices: a whole 2x2x4 slice. The times are simulated.
32 devices in a mesh: dp: 4 (over x, y), ep: 8 (over z, core).
Axes of the slice: x: 2, y: 2, z: 4, core: 2. Of those that a mesh axis runs over, the one named last changes fastest.
Arguments:
- x: bfloat16 [4, 8, 256, 3584], P('dp', 'ep'), parts along dimension 0
- expert: int32 [4, 8, 256, 2], P('dp', 'ep'), parts along dimension 0
- slot: int32 [4, 8, 256, 2], P('dp', 'ep'), parts along dimension 0
- gate: float32 [4, 8, 256, 2], P('dp', 'ep'), parts along dimension 0
- w_gate: bfloat16 [16, 3584, 4864], P('ep')
- w_up: bfloat16 [16, 3584, 4864], P('ep')
- w_down: bfloat16 [16, 4864, 3584], P('ep')
Outputs:
- y: bfloat16 [4, 8, 256, 3584], P('dp', 'ep'), parts along dimension 0
There are 4 independent parts. A program takes and returns all parts, laid end to end along the dimension named above; an argument that names none is the same for every part.
All inputs are finite; a program needn't handle non-finite values.
Results may differ from a plain program's by a relative error of at most 0.009.
Values are sent between devices in bfloat16 or wider.
A program may use at most 2 GiB of HBM per device.

v0:
```python
import jax
import jax.numpy as jnp
from jax import lax
from jax.sharding import NamedSharding, PartitionSpec as P


def einsum(form, a, b):
    return jnp.einsum(form, a.astype(jnp.float32), b.astype(jnp.float32))


def solution(mesh):
    def placed(v, *spec):
        return lax.with_sharding_constraint(v, NamedSharding(mesh, P(*spec)))

    def step(x, expert, slot, gate, w_gate, w_up, w_down):
        experts, (tokens, top) = w_gate.shape[0], expert.shape[2:]
        slots = 5 * tokens * top // (4 * experts)
        to_expert = jax.nn.one_hot(expert, experts, dtype=jnp.bfloat16)
        to_slot = jax.nn.one_hot(slot, slots, dtype=jnp.bfloat16)
        weighted = to_expert * gate[..., None].astype(jnp.bfloat16)
        dispatch = einsum("abtke,abtkc->abtec", to_expert, to_slot).astype(jnp.bfloat16)
        combine = einsum("abtke,abtkc->abtec", weighted, to_slot).astype(jnp.bfloat16)
        z = einsum("abtec,abtd->aebcd", dispatch, x).astype(jnp.bfloat16)
        z = placed(z, "dp", None, "ep", None, None)
        z = placed(z, "dp", "ep", None, None, None)
        h = jax.nn.silu(einsum("aebcd,edf->aebcf", z, w_gate))
        h = (h * einsum("aebcd,edf->aebcf", z, w_up)).astype(jnp.bfloat16)
        out = einsum("aebcf,efd->aebcd", h, w_down).astype(jnp.bfloat16)
        out = placed(out, "dp", "ep", None, None, None)
        out = placed(out, "dp", None, "ep", None, None)
        y = einsum("abtec,aebcd->abtd", combine, out)
        return y.astype(jnp.bfloat16)

    return step
```

profile of v0, /device:TPU:0, one launch (start us, length us, event | category | flops | bytes accessed | tf_op | source)
XLA Modules:
  0.0 338.3 jit_solution(1319877472779098438)
XLA Ops:
  0.0 0.0 copy-start
  0.0 0.9 copy.11
  1.0 0.8 copy.9
  1.8 2.0 convolution_convert_fusion.1
  3.8 0.0 copy-done
  3.8 1.5 convolution_convert_fusion
  5.3 108.8 %all-to-all.4 = bf16[1,8,2,1,40,3584]{5,4,2,3,0,1:T(8,128)(2,1)} all-to-all(bf16[1,8,2,1,40,3584]{5,4,2,3,0,1:T(8,128)(2,1)S(1)} %bitcast.93), channel_id=1, replica_groups=mesh['dp'=4,'ep'=8] {'ep'}, dimensions={1} | all-to-all | bytes 9175040 | tf_op jit(solution)/sharding_constraint;jit(solution)/sharding_constraint | solution.py:13
  114.2 35.8 %fusion.4 = f32[2,8,40,4864]{3,2,1,0:T(8,128)} fusion(bf16[2,3584,4864]{2,1,0:T(8,128)(2,1)} %param.4, bf16[1,8,2,1,40,3584]{5,4,2,3,0,1:T(8,128)(2,1)} %all-to-all.4), kind=kOutput, calls=%fused_computation.4 | convolution fusion | flops 22313697280 | bytes 86769664 | tf_op jit(solution)/aebcd,edf->aebcf/dot_general | solution.py:8
  150.0 35.8 %fusion.12 = bf16[2,8,40,4864]{3,2,1,0:T(8,128)(2,1)} fusion(bf16[2,3584,4864]{2,1,0:T(8,128)(2,1)} %param.5, f32[2,8,40,4864]{3,2,1,0:T(8,128)} %fusion.4, bf16[1,8,2,1,40,3584]{5,4,2,3,0,1:T(8,128)(2,1)} %all-to-all.4), kind=kOutput, calls=%fused_computation.13 | convolution fusion | flops 22332375040 | bytes 92995584 | tf_op jit(solution)/aebcd,edf->aebcf/dot_general | solution.py:8
  185.8 35.5 %fusion.18 = bf16[1,2,8,1,40,3584]{5,4,2,1,3,0:T(8,128)(2,1)} fusion(bf16[2,8,40,4864]{3,2,1,0:T(8,128)(2,1)} %fusion.12, bf16[2,4864,3584]{2,1,0:T(8,128)(2,1)} %param.6), kind=kOutput, calls=%fused_computation.16 | convolution fusion | flops 22315991040 | bytes 80543744 | tf_op jit(solution)/aebcf,efd->aebcd/dot_general | solution.py:8
  221.2 4.9 %copy.15 = bf16[1,2,8,1,40,3584]{5,4,1,3,0,2:T(8,128)(2,1)} copy(bf16[1,2,8,1,40,3584]{5,4,2,1,3,0:T(8,128)(2,1)} %fusion.18) | data formatting | bytes 9175040 | tf_op jit(solution)/sharding_constraint;jit(solution)/sharding_constraint | solution.py:13
  226.1 0.0 copy-start.1
  226.1 4.7 %all-to-all-start.1 = ((bf16[1,2,8,1,40,3584]{5,4,1,3,0,2:T(8,128)(2,1)}), bf16[1,2,8,1,40,3584]{5,4,1,3,0,2:T(8,128)(2,1)}, u32[]{:S(2)}, u32[]{:S(2)}) async-start(bf16[1,2,8,1,40,3584]{5,4,1,3,0,2:T(8,128)(2,1)} %copy.15), calls=%async_computation.1 | async-start | bytes 9175040 | tf_op jit(solution)/sharding_constraint;jit(solution)/sharding_constraint | solution.py:13
  230.8 0.0 copy-done.1
  230.9 0.1 copy.10
  231.0 2.4 convolution_convert_fusion.2
  233.4 99.5 %all-to-all-done.1 = bf16[1,2,8,1,40,3584]{5,4,1,3,0,2:T(8,128)(2,1)} async-done(((bf16[1,2,8,1,40,3584]{5,4,1,3,0,2:T(8,128)(2,1)}), bf16[1,2,8,1,40,3584]{5,4,1,3,0,2:T(8,128)(2,1)}, u32[]{:S(2)}, u32[]{:S(2)}) %all-to-all-start.1) | async-done | bytes 4587552 | tf_op jit(solution)/sharding_constraint;jit(solution)/sharding_constraint | solution.py:13
  332.9 5.3 %fusion.22 = bf16[1,1,256,3584]{3,2,1,0:T(8,128)(2,1)} fusion(bf16[16,40,3584]{2,1,0:T(8,128)(2,1)} %bitcast.25, bf16[256,16,40]{2,1,0:T(8,128)(2,1)S(1)} %convolution_convert_fusion.2), kind=kOutput, calls=%fused_computation.19 | convolution fusion | flops 1175322624 | bytes 6750208 | tf_op jit(solution)/abtec,aebcd->abtd/dot_general | solution.py:8
  (1 shorter events, 0.0 us)
Async XLA Ops:
  0.0 3.8 %copy-start = (bf16[1,1,256,3584]{3,2,1,0:T(8,128)(2,1)S(1)}, bf16[1,1,256,3584]{3,2,1,0:T(8,128)(2,1)}, u32[]{:S(2)}) copy-start(bf16[1,1,256,3584]{3,2,1,0:T(8,128)(2,1)} %param.3) | copy-start | bytes 5505028
  226.1 4.7 %copy-start.1 = (f32[1,1,256,2]{2,3,1,0:T(2,128)S(1)}, f32[1,1,256,2]{2,3,1,0:T(2,128)}, u32[]{:S(2)}) copy-start(f32[1,1,256,2]{2,3,1,0:T(2,128)} %param.1) | copy-start | bytes 6148
  226.1 106.8 %all-to-all-start.1 = ((bf16[1,2,8,1,40,3584]{5,4,1,3,0,2:T(8,128)(2,1)}), bf16[1,2,8,1,40,3584]{5,4,1,3,0,2:T(8,128)(2,1)}, u32[]{:S(2)}, u32[]{:S(2)}) async-start(bf16[1,2,8,1,40,3584]{5,4,1,3,0,2:T(8,128)(2,1)} %copy.15), calls=%async_computation.1 | async-start | bytes 9175040 | tf_op jit(solution)/sharding_constraint;jit(solution)/sharding_constraint | solution.py:13
where the time goes:
time: 339 us; the launch traced here: 338 us
  matrix products  118 us (35%)
  blocking collectives  109 us (32%)
  waiting for transfers between devices  99.5 us (29%)
  local copies, waits for them, and re-layouts  6.78 us (2%)
  starting transfers between devices  4.71 us (1%)
    dot_general x7, matrix products, einsum(): return jnp.einsum(form, a.astype(jnp.float32), b.astype(jnp.float32))  118 us
    another operation x1, blocking collectives, placed(): return lax.with_sharding_constraint(v, NamedSharding(mesh, P(*spec)))  109 us
    another operation x1, waiting for transfers between devices, placed(): return lax.with_sharding_constraint(v, NamedSharding(mesh, P(*spec)))  99.5 us
  transfers between devices with their start and end apart: 1, of which 1 were waited for; matrix products, arithmetic and copies ran while one was open for 1% of the time, Pallas kernels for 0%

commit v1 on v0

v1 whole, which is shorter than its diff:
```python
import functools

import jax
import jax.numpy as jnp
from jax import lax
from jax.experimental import pallas as pl
from jax.experimental.pallas import tpu as pltpu
from jax.sharding import PartitionSpec as P

MESH = pl.DeviceIdType.MESH
BF16, F32 = jnp.bfloat16, jnp.float32
CW = 256
KC = 512
AHEAD = 3
VMEM_BYTES = 66 * 1024 * 1024 - 2 * 1024 * 1024 - 65536


def dot(a, b):
    return jnp.dot(a, b, preferred_element_type=F32)


def dot_nt(a, b):
    return lax.dot_general(a, b, (((1,), (1,)), ((), ())), preferred_element_type=F32)


class Place:
    def __init__(self):
        self.dp = lax.axis_index("dp")
        self.ep = lax.axis_index("ep")
        self.z = lax.div(self.ep, 2)
        self.c = lax.rem(self.ep, 2)
        half = lax.div(self.z, 2)
        self.near = self.z + 1 - 2 * lax.rem(self.z, 2)
        self.far_inner = 2 - half
        self.far = [2 * (1 - half), 2 * (1 - half) + 1]
        self.inner = jnp.logical_or(self.z == 1, self.z == 2)
        self.end = jnp.logical_or(self.z == 0, self.z == 3)

    def dev(self, z, c):
        return (self.dp, 2 * z + c)

    def barrier(self):
        sem = pltpu.get_barrier_semaphore()
        for i in range(1, 8):
            peer = lax.rem(self.ep + i, 8)
            pl.semaphore_signal(sem, inc=1, device_id=(self.dp, peer), device_id_type=MESH)
        pl.semaphore_wait(sem, 7)


def route_kernel(slots, meta_ref, a_ref, cw_ref, pn_ref, pf_ref, qn_ref, qf_ref):
    me = Place()
    t = meta_ref.shape[2]
    e = [meta_ref[0], meta_ref[1]]
    s = [meta_ref[2], meta_ref[3]]
    g = [meta_ref[4], meta_ref[5]]
    src = lax.broadcasted_iota(jnp.int32, (8, t), 0)
    lane = lax.broadcasted_iota(jnp.int32, (8, t), 1)
    zs, cs = src // 2, src % 2
    near = zs + 1 - 2 * (zs % 2)
    inner, end = 2 - zs // 2, 3 - 3 * (zs // 2)
    chip = [jnp.floor(v * 0.25).astype(jnp.int32) for v in e]

    def needs(where):
        return jnp.logical_or(chip[0] == where, chip[1] == where)

    m_n, m_a = needs(near), needs(end)
    m_b = jnp.logical_and(needs(inner), jnp.logical_not(m_a))
    row = lax.broadcasted_iota(jnp.int32, (t, t), 0)
    col = lax.broadcasted_iota(jnp.int32, (t, t), 1)
    before = (row < col).astype(F32).astype(BF16)

    def count(mask):
        return dot(mask.astype(F32).astype(BF16), before).astype(jnp.int32)

    total_a = jnp.sum(m_a.astype(F32), axis=1, keepdims=True).astype(jnp.int32)
    pos_n = jnp.where(m_n, count(m_n), -1)
    pos_f = jnp.where(m_a, count(m_a), jnp.where(m_b, total_a + count(m_b), -1))
    pos = jnp.where(zs == me.z, lane, jnp.where(zs == me.near, pos_n, pos_f))

    codes = []
    for j in range(2):
        local = e[j].astype(jnp.int32) - 2 * me.ep
        hit = jnp.logical_and(local >= 0, local < 2)
        code = local * (2 * slots) + cs * slots + s[j].astype(jnp.int32) + 1
        codes.append(jnp.where(hit, code, 0).astype(F32))
    table = jnp.concatenate(codes + g, axis=0).astype(BF16)
    slot_row = lax.broadcasted_iota(jnp.int32, (4 * slots, t), 0) + 1
    slot_col = lax.broadcasted_iota(jnp.int32, (t, 4 * slots), 1) + 1
    for k in range(8):
        perm = (row == pos[k : k + 1]).astype(F32).astype(BF16)
        by_row = dot_nt(table, perm)
        by_col = dot_nt(perm, table)
        r0 = by_row[k : k + 1].astype(jnp.int32)
        r1 = by_row[8 + k : 9 + k].astype(jnp.int32)
        c0 = by_col[:, k : k + 1].astype(jnp.int32)
        c1 = by_col[:, 8 + k : 9 + k].astype(jnp.int32)
        g0, g1 = by_col[:, 16 + k : 17 + k], by_col[:, 24 + k : 25 + k]
        hit = jnp.logical_or(slot_row == r0, slot_row == r1)
        place = slice((k % 2) * t, (k % 2 + 1) * t)
        a_ref[k // 2, :, place] = hit.astype(F32).astype(BF16)
        weight = jnp.where(slot_col == c0, g0, 0.0) + jnp.where(slot_col == c1, g1, 0.0)
        cw_ref[k // 2, place, :] = weight.astype(BF16)

    eye = (row == col).astype(F32).astype(BF16)
    for pos_x, p_ref, q_ref in ((pos_n, pn_ref, qn_ref), (pos_f, pf_ref, qf_ref)):
        mine = jnp.sum(jnp.where(src == me.ep, pos_x, 0).astype(F32), axis=0, keepdims=True)
        p_ref[...] = (row == mine.astype(jnp.int32)).astype(F32).astype(BF16)
        column = dot_nt(eye, jnp.broadcast_to(mine, (8, t)).astype(BF16))[:, 0:1]
        q_ref[...] = (col == column.astype(jnp.int32)).astype(F32).astype(BF16)


def up_kernel(far_rows, end_rows, x_ref, a_ref, pn_ref, pf_ref, wg_hbm, wu_hbm, h_ref, xall, sn, sf, zbuf, gacc, uacc, wgb, wub, wsem, send_sem, recv_sem):
    me = Place()
    t, d = x_ref.shape
    ff = wg_hbm.shape[2]
    rows = zbuf.shape[1]
    n, nk = d // CW, d // KC
    tiles = ff // CW
    parts = wgb.shape[0]
    sizes = [tiles // parts + (i < tiles % parts) for i in range(parts)]
    starts = [sum(sizes[:i]) for i in range(parts)]

    def weights(u, p):
        e, k = lax.rem(u, 2), lax.div(u, 2)
        for i, (hbm, buf) in enumerate(((wg_hbm, wgb), (wu_hbm, wub))):
            yield pltpu.make_async_copy(
                hbm.at[e, pl.ds(pl.multiple_of(k * KC, KC), KC), pl.ds(starts[p] * CW, sizes[p] * CW)],
                buf.at[p, :, pl.ds(0, sizes[p] * CW)],
                wsem.at[p, i],
            )

    for p in range(parts - 1):
        for copy in weights(0, p):
            copy.start()

    def clear(j, _):
        xall[j] = jnp.zeros(xall.shape[1:], BF16)
        return 0

    lax.fori_loop(0, n, clear, 0)
    me.barrier()

    def cell(j, slot, count):
        return xall.at[j, pl.ds(pl.multiple_of(slot * t, t), count)]

    def remote(j, kind, src, slot, count, to):
        return pltpu.make_async_remote_copy(
            src_ref=src,
            dst_ref=cell(j, slot, count),
            send_sem=send_sem.at[j, kind],
            recv_sem=recv_sem.at[j, slot],
            device_id=to,
            device_id_type=MESH,
        )

    partner, nearby = me.dev(me.z, 1 - me.c), me.dev(me.near, me.c)
    own, near_slot = me.ep, 2 * me.near + me.c
    far_slots = [2 * f + me.c for f in me.far]

    def sends(j):
        cols = pl.ds(pl.multiple_of(j * CW, CW), CW)
        yield remote(j, 2, sf.at[j], own, far_rows, me.dev(me.far_inner, me.c))
        yield remote(j, 1, sn.at[j], own, end_rows, nearby)
        yield remote(j, 0, x_ref.at[:, cols], own, t, partner)

    def forward(j, kind, slot, count, to):
        return remote(j, kind, cell(j, slot, count), slot, count, to)

    def arrived(j, slot, count):
        forward(j, 0, slot, count, partner).wait_recv()

    def pack(j, _):
        cols = pl.ds(pl.multiple_of(j * CW, CW), CW)
        block = x_ref[:, cols]
        sf[j] = dot(pf_ref[:far_rows], block).astype(BF16)
        sn[j] = dot(pn_ref[:end_rows], block).astype(BF16)
        xall[j, pl.ds(pl.multiple_of(own * t, t), t)] = block
        for copy in sends(j):
            copy.start()
        return 0

    lax.fori_loop(0, AHEAD, pack, 0)

    def clear_sums(i, _):
        cols = pl.ds(pl.multiple_of(i * CW, CW), CW)
        for e in range(2):
            gacc[e, :, cols] = jnp.zeros((rows, CW), F32)
            uacc[e, :, cols] = jnp.zeros((rows, CW), F32)
        return 0

    lax.fori_loop(0, tiles, clear_sums, 0)

    def gather(k):
        for i in range(2):
            j = 2 * k + i
            arrived(j, 2 * me.z + 1 - me.c, t)
            arrived(j, 2 * me.near + 1 - me.c, end_rows)
            for f in me.far:

                @pl.when(me.inner)
                def _():
                    arrived(j, 2 * f + 1 - me.c, far_rows)

                @pl.when(me.end)
                def _():
                    arrived(j, 2 * f + 1 - me.c, end_rows)

            for zs in range(4):
                block = dot(a_ref[zs], xall[j, zs * 2 * t : (zs + 1) * 2 * t]).astype(BF16)
                size = rows // 4
                for e in range(2):
                    zbuf[e, zs * size : (zs + 1) * size, i * CW : (i + 1) * CW] = block[e * size : (e + 1) * size]

    def unit(u):
        e, k = lax.rem(u, 2), lax.div(u, 2)

        @pl.when(e == 0)
        def _():
            gather(k)

        for p in range(parts):
            for copy in weights(u, p):
                copy.wait()
            later, q = (u, p + parts - 1) if p == 0 else (u + 1, p - 1)

            @pl.when(later < 2 * nk)
            def _():
                for copy in weights(later, q):
                    copy.start()

            def tile(i, last):
                here = pl.ds(pl.multiple_of(i * CW, CW), CW)
                cols = pl.ds(pl.multiple_of((starts[p] + i) * CW, CW), CW)
                z = zbuf[e]
                gate = gacc[e, :, cols] + dot(z, wgb[p, :, here])
                up = uacc[e, :, cols] + dot(z, wub[p, :, here])
                if last:
                    h_ref[e, :, cols] = (gate * jax.nn.sigmoid(gate) * up).astype(BF16)
                else:
                    gacc[e, :, cols] = gate
                    uacc[e, :, cols] = up
                return 0

            @pl.when(k < nk - 1)
            def _():
                lax.fori_loop(0, sizes[p], lambda i, _: tile(i, False), 0)

            @pl.when(k == nk - 1)
            def _():
                lax.fori_loop(0, sizes[p], lambda i, _: tile(i, True), 0)

    def step(j, _):
        @pl.when(j + AHEAD < n)
        def _():
            pack(j + AHEAD, 0)

        @pl.when(j < n)
        def _():
            @pl.when(me.inner)
            def _():
                for i, slot in enumerate(far_slots):
                    arrived(j, slot, far_rows)
                    forward(j, 6 + i, slot, end_rows, nearby).start()
                    forward(j, 4 + i, slot, far_rows, partner).start()

            arrived(j, near_slot, end_rows)
            forward(j, 3, near_slot, end_rows, partner).start()

        @pl.when(jnp.logical_and(me.end, jnp.logical_and(j >= 1, j <= n)))
        def _():
            for i, slot in enumerate(far_slots):
                arrived(j - 1, slot, end_rows)
                forward(j - 1, 4 + i, slot, end_rows, partner).start()

        @pl.when(j >= 3)
        def _():
            unit(j - 3)

        return 0

    lax.fori_loop(0, n + 3, step, 0)

    def drain(j, _):
        for copy in sends(j):
            copy.wait_send()
        forward(j, 3, near_slot, end_rows, partner).wait_send()

        @pl.when(me.inner)
        def _():
            for i, slot in enumerate(far_slots):
                forward(j, 6 + i, slot, end_rows, nearby).wait_send()
                forward(j, 4 + i, slot, far_rows, partner).wait_send()

        @pl.when(me.end)
        def _():
            for i, slot in enumerate(far_slots):
                forward(j, 4 + i, slot, end_rows, partner).wait_send()

        return 0

    lax.fori_loop(0, n, drain, 0)


def down_kernel(far_rows, end_rows, h_ref, cw_ref, qn_ref, qf_ref, wd_hbm, y_ref, o, yd, yn, yf, yr, sd, sn, sf, wdb, wsem, send_sem, dsem, nsem, fsem, rsem):
    me = Place()
    t, d = y_ref.shape
    ff = wd_hbm.shape[1]
    rows = h_ref.shape[1]
    size = rows // 4
    n = d // CW
    depth = wdb.shape[0]
    lag = 5

    def weights(q):
        cols = pl.ds(pl.multiple_of(q * CW, CW), CW)
        slot = lax.rem(q, depth)
        for e in range(2):
            yield pltpu.make_async_copy(wd_hbm.at[e, :, cols], wdb.at[slot, e], wsem.at[slot, e])

    for q in range(depth - 1):
        for copy in weights(q):
            copy.start()
    me.barrier()

    partner, nearby = me.dev(me.z, 1 - me.c), me.dev(me.near, me.c)

    def remote(q, kind, src, dst, recv, to):
        return pltpu.make_async_remote_copy(
            src_ref=src, dst_ref=dst, send_sem=send_sem.at[q, kind], recv_sem=recv, device_id=to, device_id_type=MESH
        )

    def to_partner(q):
        return remote(q, 0, sd.at[q], yd.at[q], dsem.at[q], partner)

    def to_near(q):
        return remote(q, 1, sn.at[q], yn.at[q], nsem.at[q], nearby)

    def relay(q, i):
        return remote(q, 2 + i, sf.at[q, i, pl.ds(0, end_rows)], yr.at[q, i], rsem.at[q, i], nearby)

    def to_far(q, i):
        return remote(q, 2 + i, sf.at[q, i], yf.at[q], fsem.at[q], me.dev(me.far[i], me.c))

    def part(q, zs, c, count):
        return dot(cw_ref[zs, pl.ds(pl.multiple_of(c * t, t), count), :], o[q, zs])

    def both(q, zs, count):
        other = yd[q, pl.ds(pl.multiple_of(zs * t, t), count)].astype(F32)
        return part(q, zs, me.c, count) + other

    def step(q, _):
        @pl.when(q < n)
        def _():
            for copy in weights(q):
                copy.wait()

            @pl.when(q + depth - 1 < n)
            def _():
                for copy in weights(q + depth - 1):
                    copy.start()

            slot = lax.rem(q, depth)
            for e in range(2):
                block = dot(h_ref[e], wdb[slot, e]).astype(BF16)
                for zs in range(4):
                    o[q, zs, e * size : (e + 1) * size] = block[zs * size : (zs + 1) * size]
            for zs in range(4):
                sd[q, zs * t : (zs + 1) * t] = part(q, zs, 1 - me.c, t).astype(BF16)
            to_partner(q).start()

        @pl.when(jnp.logical_and(q >= 1, q <= n))
        def _():
            r = q - 1
            to_partner(r).wait_recv()

            @pl.when(me.end)
            def _():
                for i, f in enumerate(me.far):
                    sf[r, i, 0:end_rows] = both(r, f, end_rows).astype(BF16)
                    relay(r, i).start()

            sn[r] = both(r, me.near, end_rows).astype(BF16)
            to_near(r).start()

        @pl.when(jnp.logical_and(me.inner, jnp.logical_and(q >= 2, q <= n + 1)))
        def _():
            r = q - 2
            for i, f in enumerate(me.far):
                relay(r, i).wait_recv()
                total = both(r, f, far_rows)
                sf[r, i, 0:end_rows] = (total[:end_rows] + yr[r, i].astype(F32)).astype(BF16)
                if far_rows > end_rows:
                    sf[r, i, end_rows:far_rows] = total[end_rows:].astype(BF16)
                to_far(r, i).start()

        @pl.when(q >= lag)
        def _():
            r = q - lag
            to_near(r).wait_recv()
            to_far(r, 0).wait_recv()
            total = both(r, me.z, t)
            total += dot(qn_ref[:, :end_rows], yn[r])
            total += dot(qf_ref[:, :far_rows], yf[r])
            y_ref[:, pl.ds(pl.multiple_of(r * CW, CW), CW)] = total.astype(BF16)

        return 0

    lax.fori_loop(0, n + lag, step, 0)

    def drain(q, _):
        to_partner(q).wait_send()
        to_near(q).wait_send()

        @pl.when(me.end)
        def _():
            for i in range(2):
                relay(q, i).wait_send()

        @pl.when(me.inner)
        def _():
            for i in range(2):
                to_far(q, i).wait_send()

        return 0

    lax.fori_loop(0, n, drain, 0)


def up_call(x, a, pn, pf, w_gate, w_up, slots, far_rows, end_rows, ident):
    t, d = x.shape
    ff = w_gate.shape[2]
    n, rows = d // CW, 8 * slots
    tiles = ff // CW
    parts = min(4, tiles)
    wide = -(-tiles // parts) * CW
    vmem, hbm = pl.BlockSpec(memory_space=pltpu.VMEM), pl.BlockSpec(memory_space=pl.ANY)
    return pl.pallas_call(
        functools.partial(up_kernel, far_rows, end_rows),
        out_shape=jax.ShapeDtypeStruct((2, rows, ff), BF16),
        in_specs=[vmem] * 4 + [hbm] * 2,
        out_specs=vmem,
        scratch_shapes=[
            pltpu.VMEM((n, 8 * t, CW), BF16),
            pltpu.VMEM((n, end_rows, CW), BF16),
            pltpu.VMEM((n, far_rows, CW), BF16),
            pltpu.VMEM((2, rows, KC), BF16),
            pltpu.VMEM((2, rows, ff), F32),
            pltpu.VMEM((2, rows, ff), F32),
            pltpu.VMEM((parts, KC, wide), BF16),
            pltpu.VMEM((parts, KC, wide), BF16),
            pltpu.SemaphoreType.DMA((parts, 2)),
            pltpu.SemaphoreType.DMA((n, 8)),
            pltpu.SemaphoreType.DMA((n, 8)),
        ],
        compiler_params=pltpu.CompilerParams(collective_id=ident, has_side_effects=True, vmem_limit_bytes=VMEM_BYTES),
        name=f"up_{far_rows}_{end_rows}",
    )(x, a, pn, pf, w_gate, w_up)


def down_call(h, cw, qn, qf, w_down, far_rows, end_rows, ident):
    _, rows, ff = h.shape
    d, t = w_down.shape[2], qn.shape[0]
    n = d // CW
    vmem, hbm = pl.BlockSpec(memory_space=pltpu.VMEM), pl.BlockSpec(memory_space=pl.ANY)
    return pl.pallas_call(
        functools.partial(down_kernel, far_rows, end_rows),
        out_shape=jax.ShapeDtypeStruct((t, d), BF16),
        in_specs=[vmem] * 4 + [hbm],
        out_specs=vmem,
        scratch_shapes=[
            pltpu.VMEM((n, 4, rows // 2, CW), BF16),
            pltpu.VMEM((n, 4 * t, CW), BF16),
            pltpu.VMEM((n, end_rows, CW), BF16),
            pltpu.VMEM((n, far_rows, CW), BF16),
            pltpu.VMEM((n, 2, end_rows, CW), BF16),
            pltpu.VMEM((n, 4 * t, CW), BF16),
            pltpu.VMEM((n, end_rows, CW), BF16),
            pltpu.VMEM((n, 2, far_rows, CW), BF16),
            pltpu.VMEM((3, 2, ff, CW), BF16),
            pltpu.SemaphoreType.DMA((3, 2)),
            pltpu.SemaphoreType.DMA((n, 4)),
            pltpu.SemaphoreType.DMA((n,)),
            pltpu.SemaphoreType.DMA((n,)),
            pltpu.SemaphoreType.DMA((n,)),
            pltpu.SemaphoreType.DMA((n, 2)),
        ],
        compiler_params=pltpu.CompilerParams(collective_id=ident, has_side_effects=True, vmem_limit_bytes=VMEM_BYTES),
        name=f"down_{far_rows}_{end_rows}",
    )(h, cw, qn, qf, w_down)


def route_call(meta, slots):
    t = meta.shape[2]
    vmem = pl.BlockSpec(memory_space=pltpu.VMEM)
    square = jax.ShapeDtypeStruct((t, t), BF16)
    return pl.pallas_call(
        functools.partial(route_kernel, slots),
        out_shape=[
            jax.ShapeDtypeStruct((4, 4 * slots, 2 * t), BF16),
            jax.ShapeDtypeStruct((4, 2 * t, 4 * slots), BF16),
            square,
            square,
            square,
            square,
        ],
        in_specs=[vmem],
        out_specs=[vmem] * 6,
        name="route",
    )(meta)


def solution(mesh):
    def body(x, expert, slot, gate, w_gate, w_up, w_down):
        x, expert, slot, gate = x[0, 0], expert[0, 0], slot[0, 0], gate[0, 0]
        t = x.shape[0]
        slots = 5 * t * 2 // (4 * 16)
        kept = jnp.where(slot < slots, expert, -1)
        meta = jnp.concatenate([kept.T.astype(F32), jnp.minimum(slot, slots).T.astype(F32), gate.T], axis=0)
        meta = lax.all_gather(meta, "ep", axis=1)
        a, cw, pn, pf, qn, qf = route_call(meta, slots)
        far_rows, end_rows = t, 4 * slots
        h = up_call(x, a, pn, pf, w_gate, w_up, slots, far_rows, end_rows, 1)
        y = down_call(h, cw, qn, qf, w_down, far_rows, end_rows, 2)
        return y[None, None]

    data, weight = P("dp", "ep", None, None), P("ep", None, None)
    return jax.shard_map(
        body,
        mesh=mesh,
        in_specs=(data, data, data, data, weight, weight, weight),
        out_specs=data,
        check_vma=False,
    )
```

time: 339 us -> 261 us (0.77)
  Pallas kernels: 0 us -> 241 us
  matrix products: 118 us -> 0 us
  waiting for transfers between devices: 99.5 us -> 0 us
  blocking collectives: 109 us -> 15.6 us
  starting transfers between devices: 4.71 us -> 0 us
    pallas_call x0 -> x3, Pallas kernels: none -> 241 us  [the longest x1 142 us: up_call(): pl.pallas_call(functools.partial(up_kernel, far_rows, end_rows), out_shap...]
    dot_general x7 -> x0, matrix products: 118 us -> none  [einsum(): return jnp.einsum(form, a.astype(jnp.float32), b.astype(jnp.float32))]
    another operation x1 -> x0, blocking collectives: 109 us -> none  [placed(): return lax.with_sharding_constraint(v, NamedSharding(mesh, P(*spec)))]
    another operation x1 -> x0, waiting for transfers between devices: 99.5 us -> none  [placed(): return lax.with_sharding_constraint(v, NamedSharding(mesh, P(*spec)))]
    all_gather x0 -> x1, blocking collectives: none -> 15.6 us  [body(): meta = lax.all_gather(meta, 'ep', axis=1)]
    another operation x1 -> x0, local copies, waits for them, and re-layouts: 4.87 us -> none  [placed(): return lax.with_sharding_constraint(v, NamedSharding(mesh, P(*spec)))]
    another operation x1 -> x0, starting transfers between devices: 4.71 us -> none  [placed(): return lax.with_sharding_constraint(v, NamedSharding(mesh, P(*spec)))]
  transfers between devices with their start and end apart: 1 -> 0, of which waited for: 1 -> 0; matrix products, arithmetic and copies ran while one was open for 1% -> 0% of each run, Pallas kernels for 0% -> 0%
where the time goes in v1:
time: 261 us
  Pallas kernels  241 us (92%)
  blocking collectives  15.6 us (6%)
  local copies, waits for them, and re-layouts  3.48 us (1%)
    pallas_call x1, Pallas kernels, up_call(): pl.pallas_call(functools.partial(up_kernel, far_rows, end_rows), out_shap...  142 us
    pallas_call x1, Pallas kernels, down_call(): pl.pallas_call(functools.partial(down_kernel, far_rows, end_rows), out_sh...  95.1 us
    all_gather x1, blocking collectives, body(): meta = lax.all_gather(meta, 'ep', axis=1)  15.6 us

profile of v1, /device:TPU:0, one launch (start us, length us, event | category | flops | bytes accessed | tf_op | source)
XLA Modules:
  0.0 261.1 jit_solution(17163015256217257557)
XLA Ops:
  0.0 0.7 fusion.1
  0.7 0.7 pad_maximum_fusion
  1.4 15.6 %all-gather = f32[6,2048]{1,0:T(8,128)S(1)} all-gather(f32[6,256]{1,0:T(8,128)S(1)} %pad_maximum_fusion), channel_id=2, replica_groups=mesh['dp'=4,'ep'=8] {'ep'}, dimensions={1}, use_global_device_ids=true | all-gather | bytes 55296 | tf_op jit(solution)/shard_map/all_gather | solution.py:519
  17.0 0.6 copy.10
  17.6 3.9 %route.1 = (bf16[4,160,512]{2,1,0:T(8,128)(2,1)}, bf16[4,512,160]{2,1,0:T(8,128)(2,1)}, bf16[256,256]{1,0:T(8,128)(2,1)}, bf16[256,256]{1,0:T(8,128)(2,1)}, bf16...) custom-call(f32[6,8,256]{2,1,0:T(8,128)} %bitcast.20), custom_call_target="tpu_custom_call" | custom-call | tf_op jit(solution)/shard_map/route/pallas_call | solution.py:496
  21.5 141.6 %up_256_160.1.h_ref = bf16[2,320,4864]{2,1,0:T(8,128)(2,1)} custom-call(bf16[256,3584]{1,0:T(8,128)(2,1)} %bitcast.18, bf16[4,160,512]{2,1,0:T(8,128)(2,1)} %get-tuple-element.11.a_ref, bf16[256,256]{1,0:T(8,128)(2,1)} %get-tuple-element.12.pn_ref, bf16[256,256]{1,0:T(8,128)(2,1)} %get-tuple-element.13.pf_ref, bf16[2,3584,4864]{2,1,0:T(8,128)(2,1)} %wg_hbm.1, ...), custom_call_target="tpu_custom_call" | custom-call | tf_op jit(solution)/shard_map/up_256_160/pallas_call | solution.py:437
  163.1 95.1 %down_256_160.1 = bf16[256,3584]{1,0:T(8,128)(2,1)} custom-call(bf16[2,320,4864]{2,1,0:T(8,128)(2,1)} %up_256_160.1.h_ref, bf16[4,512,160]{2,1,0:T(8,128)(2,1)} %get-tuple-element.14.cw_ref, bf16[256,256]{1,0:T(8,128)(2,1)} %get-tuple-element.15.qn_ref, bf16[256,256]{1,0:T(8,128)(2,1)} %get-tuple-element.16.qf_ref, bf16[2,4864,3584]{2,1,0:T(8,128)(2,1)} %wd_hbm.1), custom_call_target="tpu_custom_call" | custom-call | tf_op jit(solution)/shard_map/down_256_160/pallas_call | solution.py:465
  258.2 2.8 %copy.12 = bf16[1,1,256,3584]{3,2,1,0:T(8,128)(2,1)} copy(bf16[1,1,256,3584]{3,2,1,0:T(8,128)(2,1)} %bitcast.17) | data formatting | bytes 3670016

commit v2 on v1

--- a/solution.py
+++ b/solution.py
@@ -47,12 +47,54 @@
         pl.semaphore_wait(sem, 7)
 
 
-def route_kernel(slots, meta_ref, a_ref, cw_ref, pn_ref, pf_ref, qn_ref, qf_ref):
+def route_kernel(slots, sizes, several, expert_ref, slot_ref, gate_ref, a_ref, cw_ref, pn_ref, pf_ref, qn_ref, qf_ref, pick_ref, mine, every, top, tops, send_sem, recv_sem, top_send, top_recv):
     me = Place()
-    t = meta_ref.shape[2]
-    e = [meta_ref[0], meta_ref[1]]
-    s = [meta_ref[2], meta_ref[3]]
-    g = [meta_ref[4], meta_ref[5]]
+    t = expert_ref.shape[1]
+    slot = slot_ref[...]
+    mine[0:2] = jnp.where(slot < slots, expert_ref[...], -1).astype(F32)
+    mine[2:4] = jnp.minimum(slot, slots).astype(F32)
+    mine[4:6] = gate_ref[...]
+    mine[6:8] = jnp.zeros((2, t), F32)
+
+    barrier = pltpu.get_barrier_semaphore()
+    peers = [(me.dp, lax.rem(me.ep + i, 8)) for i in range(1, 8)]
+    groups = [(lax.rem(me.dp + i, 4), me.ep) for i in range(1, 4)]
+    if not several:
+        groups = []
+    for peer in peers + groups:
+        pl.semaphore_signal(barrier, inc=1, device_id=peer, device_id_type=MESH)
+    pl.semaphore_wait(barrier, len(peers) + len(groups))
+
+    def table_to(i):
+        return pltpu.make_async_remote_copy(
+            src_ref=mine,
+            dst_ref=every.at[me.ep],
+            send_sem=send_sem.at[i],
+            recv_sem=recv_sem.at[me.ep],
+            device_id=peers[i],
+            device_id_type=MESH,
+        )
+
+    def table_from(i):
+        source = lax.rem(me.ep + 8 - i, 8)
+        return pltpu.make_async_remote_copy(
+            src_ref=mine,
+            dst_ref=every.at[source],
+            send_sem=send_sem.at[0],
+            recv_sem=recv_sem.at[source],
+            device_id=peers[0],
+            device_id_type=MESH,
+        )
+
+    for i in range(7):
+        table_to(i).start()
+    every[me.ep] = mine[...]
+    for i in range(1, 8):
+        table_from(i).wait_recv()
+
+    e = [every[:, 0, :], every[:, 1, :]]
+    s = [every[:, 2, :], every[:, 3, :]]
+    g = [every[:, 4, :], every[:, 5, :]]
     src = lax.broadcasted_iota(jnp.int32, (8, t), 0)
     lane = lax.broadcasted_iota(jnp.int32, (8, t), 1)
     zs, cs = src // 2, src % 2
@@ -75,6 +117,27 @@
     total_a = jnp.sum(m_a.astype(F32), axis=1, keepdims=True).astype(jnp.int32)
     pos_n = jnp.where(m_n, count(m_n), -1)
     pos_f = jnp.where(m_a, count(m_a), jnp.where(m_b, total_a + count(m_b), -1))
+    def most(mask):
+        return jnp.max(jnp.sum(mask.astype(F32), axis=1, keepdims=True), axis=0, keepdims=True)
+
+    far_top = most(jnp.logical_or(m_a, m_b))
+    end_top = jnp.maximum(most(m_a), most(m_n))
+    which = lax.broadcasted_iota(jnp.int32, (8, 128), 0)
+    top[...] = jnp.where(which == 0, far_top, end_top)
+
+    def top_copy(i, slot):
+        return pltpu.make_async_remote_copy(
+            src_ref=top,
+            dst_ref=tops.at[slot],
+            send_sem=top_send.at[i],
+            recv_sem=top_recv.at[slot],
+            device_id=groups[i],
+            device_id_type=MESH,
+        )
+
+    for i in range(len(groups)):
+        top_copy(i, i).start()
+
     pos = jnp.where(zs == me.z, lane, jnp.where(zs == me.near, pos_n, pos_f))
 
     codes = []
@@ -103,10 +166,24 @@
 
     eye = (row == col).astype(F32).astype(BF16)
     for pos_x, p_ref, q_ref in ((pos_n, pn_ref, qn_ref), (pos_f, pf_ref, qf_ref)):
-        mine = jnp.sum(jnp.where(src == me.ep, pos_x, 0).astype(F32), axis=0, keepdims=True)
-        p_ref[...] = (row == mine.astype(jnp.int32)).astype(F32).astype(BF16)
-        column = dot_nt(eye, jnp.broadcast_to(mine, (8, t)).astype(BF16))[:, 0:1]
+        order = jnp.sum(jnp.where(src == me.ep, pos_x, 0).astype(F32), axis=0, keepdims=True)
+        p_ref[...] = (row == order.astype(jnp.int32)).astype(F32).astype(BF16)
+        column = dot_nt(eye, jnp.broadcast_to(order, (8, t)).astype(BF16))[:, 0:1]
         q_ref[...] = (col == column.astype(jnp.int32)).astype(F32).astype(BF16)
+
+    limit = top[...]
+    for i in range(len(groups)):
+        top_copy(i, i).wait_recv()
+        limit = jnp.maximum(limit, tops[i])
+    far_max, end_max = limit[0:1], limit[1:2]
+    pick = jnp.full((1, 128), len(sizes) - 1, jnp.int32)
+    for i, (far_rows, end_rows) in reversed(list(enumerate(sizes[:-1]))):
+        pick = jnp.where(jnp.logical_and(far_max <= far_rows, end_max <= end_rows), i, pick)
+    pick_ref[...] = jnp.broadcast_to(pick, (8, 128))
+    for i in range(7):
+        table_to(i).wait_send()
+    for i in range(len(groups)):
+        top_copy(i, i).wait_send()
 
 
 def up_kernel(far_rows, end_rows, x_ref, a_ref, pn_ref, pf_ref, wg_hbm, wu_hbm, h_ref, xall, sn, sf, zbuf, gacc, uacc, wgb, wub, wsem, send_sem, recv_sem):
@@ -218,19 +295,22 @@
         def _():
             gather(k)
 
-        for p in range(parts):
+        def tiles_of(p, last):
             for copy in weights(u, p):
                 copy.wait()
             later, q = (u, p + parts - 1) if p == 0 else (u + 1, p - 1)
 
-            @pl.when(later < 2 * nk)
-            def _():
+            def start():
                 for copy in weights(later, q):
                     copy.start()
 
-            def tile(i, last):
-                here = pl.ds(pl.multiple_of(i * CW, CW), CW)
-                cols = pl.ds(pl.multiple_of((starts[p] + i) * CW, CW), CW)
+            if p > 0 and last:
+                pl.when(later < 2 * nk)(start)
+            else:
+                start()
+            for i in range(sizes[p]):
+                here = pl.ds(i * CW, CW)
+                cols = pl.ds((starts[p] + i) * CW, CW)
                 z = zbuf[e]
                 gate = gacc[e, :, cols] + dot(z, wgb[p, :, here])
                 up = uacc[e, :, cols] + dot(z, wub[p, :, here])
@@ -239,15 +319,16 @@
                 else:
                     gacc[e, :, cols] = gate
                     uacc[e, :, cols] = up
-                return 0
-
-            @pl.when(k < nk - 1)
-            def _():
-                lax.fori_loop(0, sizes[p], lambda i, _: tile(i, False), 0)
-
-            @pl.when(k == nk - 1)
-            def _():
-                lax.fori_loop(0, sizes[p], lambda i, _: tile(i, True), 0)
+
+        @pl.when(k < nk - 1)
+        def _():
+            for p in range(parts):
+                tiles_of(p, False)
+
+        @pl.when(k == nk - 1)
+        def _():
+            for p in range(parts):
+                tiles_of(p, True)
 
     def step(j, _):
         @pl.when(j + AHEAD < n)
@@ -489,12 +570,12 @@
     )(h, cw, qn, qf, w_down)
 
 
-def route_call(meta, slots):
-    t = meta.shape[2]
+def route_call(expert, slot, gate, slots, sizes, several):
+    t = expert.shape[1]
     vmem = pl.BlockSpec(memory_space=pltpu.VMEM)
     square = jax.ShapeDtypeStruct((t, t), BF16)
     return pl.pallas_call(
-        functools.partial(route_kernel, slots),
+        functools.partial(route_kernel, slots, sizes, several),
         out_shape=[
             jax.ShapeDtypeStruct((4, 4 * slots, 2 * t), BF16),
             jax.ShapeDtypeStruct((4, 2 * t, 4 * slots), BF16),
@@ -502,11 +583,23 @@
             square,
             square,
             square,
+            jax.ShapeDtypeStruct((8, 128), jnp.int32),
         ],
-        in_specs=[vmem],
-        out_specs=[vmem] * 6,
+        in_specs=[vmem] * 3,
+        out_specs=[vmem] * 7,
+        scratch_shapes=[
+            pltpu.VMEM((8, t), F32),
+            pltpu.VMEM((8, 8, t), F32),
+            pltpu.VMEM((8, 128), F32),
+            pltpu.VMEM((3, 8, 128), F32),
+            pltpu.SemaphoreType.DMA((7,)),
+            pltpu.SemaphoreType.DMA((8,)),
+            pltpu.SemaphoreType.DMA((3,)),
+            pltpu.SemaphoreType.DMA((3,)),
+        ],
+        compiler_params=pltpu.CompilerParams(collective_id=0, has_side_effects=True),
         name="route",
-    )(meta)
+    )(expert, slot, gate)
 
 
 def solution(mesh):
@@ -514,13 +607,18 @@
         x, expert, slot, gate = x[0, 0], expert[0, 0], slot[0, 0], gate[0, 0]
         t = x.shape[0]
         slots = 5 * t * 2 // (4 * 16)
-        kept = jnp.where(slot < slots, expert, -1)
-        meta = jnp.concatenate([kept.T.astype(F32), jnp.minimum(slot, slots).T.astype(F32), gate.T], axis=0)
-        meta = lax.all_gather(meta, "ep", axis=1)
-        a, cw, pn, pf, qn, qf = route_call(meta, slots)
-        far_rows, end_rows = t, 4 * slots
-        h = up_call(x, a, pn, pf, w_gate, w_up, slots, far_rows, end_rows, 1)
-        y = down_call(h, cw, qn, qf, w_down, far_rows, end_rows, 2)
+        sizes = [(160, 112), (192, 144), (t, 4 * slots)]
+        a, cw, pn, pf, qn, qf, pick = route_call(expert.T, slot.T, gate.T, slots, sizes, mesh.shape["dp"] > 1)
+
+        def branch(i):
+            def run(x, w_gate, w_up, w_down):
+                far_rows, end_rows = sizes[i]
+                h = up_call(x, a, pn, pf, w_gate, w_up, slots, far_rows, end_rows, 1 + 2 * i)
+                return down_call(h, cw, qn, qf, w_down, far_rows, end_rows, 2 + 2 * i)
+
+            return run
+
+        y = lax.switch(pick[0, 0], [branch(i) for i in range(len(sizes))], x, w_gate, w_up, w_down)
         return y[None, None]
 
     data, weight = P("dp", "ep", None, None), P("ep", None, None)

time: 261 us -> 182 us (0.70)
  Pallas kernels: 241 us -> 177 us
  blocking collectives: 15.6 us -> 0 us
    pallas_call x1, Pallas kernels: 142 us -> 93.6 us  [up_call(): pl.pallas_call(functools.partial(up_kernel, far_rows, end_rows), out_shap...]
    pallas_call x1, Pallas kernels: 95.1 us -> 69.1 us  [down_call(): pl.pallas_call(functools.partial(down_kernel, far_rows, end_rows), out_sh...]
    all_gather x1 -> x0, blocking collectives: 15.6 us -> none  [body(): meta = lax.all_gather(meta, 'ep', axis=1)]
    pallas_call x1, Pallas kernels: 3.88 us -> 14.6 us  [route_call(): pl.pallas_call(functools.partial(route_kernel, slots, sizes, several), ou...]
where the time goes in v2:
time: 182 us
  Pallas kernels  177 us (97%)
  local copies, waits for them, and re-layouts  4.04 us (2%)
    pallas_call x1, Pallas kernels, up_call(): pl.pallas_call(functools.partial(up_kernel, far_rows, end_rows), out_shap...  93.6 us
    pallas_call x1, Pallas kernels, down_call(): pl.pallas_call(functools.partial(down_kernel, far_rows, end_rows), out_sh...  69.1 us
    pallas_call x1, Pallas kernels, route_call(): pl.pallas_call(functools.partial(route_kernel, slots, sizes, several), ou...  14.6 us

profile of v2, /device:TPU:0, one launch (start us, length us, event | category | flops | bytes accessed | tf_op | source)
XLA Modules:
  0.0 182.2 jit_solution(10400819557822592602)
XLA Ops:
  0.0 14.6 %route.1 = (bf16[4,160,512]{2,1,0:T(8,128)(2,1)}, bf16[4,512,160]{2,1,0:T(8,128)(2,1)}, bf16[256,256]{1,0:T(8,128)(2,1)}, bf16[256,256]{1,0:T(8,128)(2,1)}, bf16...) custom-call(s32[2,256]{1,0:T(2,128)} %bitcast.20, s32[2,256]{1,0:T(2,128)} %bitcast.21, ...), custom_call_target="tpu_custom_call" | custom-call | tf_op jit(solution)/shard_map/route/pallas_call | solution.py:577
  14.6 1.2 slice.3
  16.4 162.9 %conditional.1 = (bf16[1,1,256,3584]{3,2,1,0:T(8,128)(2,1)}) conditional(s32[]{:T(128)} %bitcast.9, (bf16[256,3584]{1,0:T(8,128)(2,1)}, bf16[4,160,512]{2,1,0:T(8,128)(2,1)}, bf16[256,256]{1,0:T(8,128)(2,1)}, bf16[256,256]{1,0:T(8,128)(2,1)}, bf16[2,3584,4864]{2,1,0:T(8,128)(2,1)}, /*index=5*/bf16[2,3584,4864]{2,1,0:T(8,128)(2,1)}, ...), branch_computations={%region_0.0_spmd, %region_1.0_spmd, %region_2.0_spmd} | conditional | bytes 8 | solution.py:621
  16.4 93.6 %up_160_112.1.h_ref = bf16[2,320,4864]{2,1,0:T(8,128)(2,1)} custom-call(bf16[256,3584]{1,0:T(8,128)(2,1)} %get-tuple-element.70.x_ref, bf16[4,160,512]{2,1,0:T(8,128)(2,1)} %get-tuple-element.71.a_ref, bf16[256,256]{1,0:T(8,128)(2,1)} %get-tuple-element.72.pn_ref, bf16[256,256]{1,0:T(8,128)(2,1)} %get-tuple-element.73.pf_ref, ...), custom_call_target="tpu_custom_call" | custom-call | tf_op jit(solution)/shard_map/cond/branch_0_fun/up_160_112/pallas_call | solution.py:518
  110.0 69.1 %down_160_112.1 = bf16[256,3584]{1,0:T(8,128)(2,1)} custom-call(bf16[2,320,4864]{2,1,0:T(8,128)(2,1)} %up_160_112.1.h_ref, bf16[4,512,160]{2,1,0:T(8,128)(2,1)} %get-tuple-element.76.cw_ref, bf16[256,256]{1,0:T(8,128)(2,1)} %get-tuple-element.77.qn_ref, bf16[256,256]{1,0:T(8,128)(2,1)} %get-tuple-element.78.qf_ref, ...), custom_call_target="tpu_custom_call" | custom-call | tf_op jit(solution)/shard_map/cond/branch_0_fun/down_160_112/pallas_call | solution.py:546
  179.3 2.8 %copy.15 = bf16[1,1,256,3584]{3,2,1,0:T(8,128)(2,1)} copy(bf16[1,1,256,3584]{3,2,1,0:T(8,128)(2,1)} %get-tuple-element.114) | data formatting | bytes 3670016

commit v3 on v2

--- a/solution.py
+++ b/solution.py
@@ -12,7 +12,7 @@
 CW = 256
 KC = 512
 AHEAD = 3
-VMEM_BYTES = 66 * 1024 * 1024 - 2 * 1024 * 1024 - 65536
+VMEM_BYTES = 67043328
 
 
 def dot(a, b):
@@ -39,23 +39,88 @@
     def dev(self, z, c):
         return (self.dp, 2 * z + c)
 
-    def barrier(self):
-        sem = pltpu.get_barrier_semaphore()
+    def greet(self, sem):
         for i in range(1, 8):
             peer = lax.rem(self.ep + i, 8)
             pl.semaphore_signal(sem, inc=1, device_id=(self.dp, peer), device_id_type=MESH)
-        pl.semaphore_wait(sem, 7)
-
-
-def route_kernel(slots, sizes, several, expert_ref, slot_ref, gate_ref, a_ref, cw_ref, pn_ref, pf_ref, qn_ref, qf_ref, pick_ref, mine, every, top, tops, send_sem, recv_sem, top_send, top_recv):
+
+
+class Packs:
+    def __init__(self, me, every):
+        t = every.shape[2]
+        self.e = [every[:, 0, :], every[:, 1, :]]
+        self.s = [every[:, 2, :], every[:, 3, :]]
+        self.g = [every[:, 4, :], every[:, 5, :]]
+        self.src = lax.broadcasted_iota(jnp.int32, (8, t), 0)
+        zs = self.src // 2
+        chip = [jnp.floor(v * 0.25).astype(jnp.int32) for v in self.e]
+
+        def needs(where):
+            return jnp.logical_or(chip[0] == where, chip[1] == where)
+
+        self.m_n = needs(zs + 1 - 2 * (zs % 2))
+        self.m_a = needs(3 - 3 * (zs // 2))
+        self.m_b = jnp.logical_and(needs(2 - zs // 2), jnp.logical_not(self.m_a))
+
+    def order(self, me):
+        t = self.src.shape[1]
+        self.row = lax.broadcasted_iota(jnp.int32, (t, t), 0)
+        self.col = lax.broadcasted_iota(jnp.int32, (t, t), 1)
+        before = (self.row < self.col).astype(F32).astype(BF16)
+
+        def count(mask):
+            return dot(mask.astype(F32).astype(BF16), before).astype(jnp.int32)
+
+        total_a = jnp.sum(self.m_a.astype(F32), axis=1, keepdims=True).astype(jnp.int32)
+        self.pos_n = jnp.where(self.m_n, count(self.m_n), -1)
+        self.pos_f = jnp.where(self.m_a, count(self.m_a), jnp.where(self.m_b, total_a + count(self.m_b), -1))
+
+    def own(self, me, pos):
+        return jnp.sum(jnp.where(self.src == me.ep, pos, 0).astype(F32), axis=0, keepdims=True)
+
+    def packers(self, me, pn_ref, pf_ref):
+        for pos, p_ref in ((self.pos_n, pn_ref), (self.pos_f, pf_ref)):
+            p_ref[...] = (self.row == self.own(me, pos).astype(jnp.int32)).astype(F32).astype(BF16)
+
+    def matrices(self, me, slots, a_ref, cw_ref, qn_ref, qf_ref):
+        t = self.src.shape[1]
+        row, col, src = self.row, self.col, self.src
+        zs, cs = src // 2, src % 2
+        lane = lax.broadcasted_iota(jnp.int32, (8, t), 1)
+        pos = jnp.where(zs == me.z, lane, jnp.where(zs == me.near, self.pos_n, self.pos_f))
+        codes = []
+        for j in range(2):
+            local = self.e[j].astype(jnp.int32) - 2 * me.ep
+            hit = jnp.logical_and(local >= 0, local < 2)
+            code = local * (2 * slots) + cs * slots + self.s[j].astype(jnp.int32) + 1
+            codes.append(jnp.where(hit, code, 0).astype(F32))
+        table = jnp.concatenate(codes + self.g, axis=0).astype(BF16)
+        slot_row = lax.broadcasted_iota(jnp.int32, (4 * slots, t), 0) + 1
+        slot_col = lax.broadcasted_iota(jnp.int32, (t, 4 * slots), 1) + 1
+        for k in range(8):
+            perm = (row == pos[k : k + 1]).astype(F32).astype(BF16)
+            by_row = dot_nt(table, perm)
+            by_col = dot_nt(perm, table)
+            r0 = by_row[k : k + 1].astype(jnp.int32)
+            r1 = by_row[8 + k : 9 + k].astype(jnp.int32)
+            c0 = by_col[:, k : k + 1].astype(jnp.int32)
+            c1 = by_col[:, 8 + k : 9 + k].astype(jnp.int32)
+            g0, g1 = by_col[:, 16 + k : 17 + k], by_col[:, 24 + k : 25 + k]
+            hit = jnp.logical_or(slot_row == r0, slot_row == r1)
+            place = slice((k % 2) * t, (k % 2 + 1) * t)
+            a_ref[k // 2, :, place] = hit.astype(F32).astype(BF16)
+            weight = jnp.where(slot_col == c0, g0, 0.0) + jnp.where(slot_col == c1, g1, 0.0)
+            cw_ref[k // 2, place, :] = weight.astype(BF16)
+        eye = (row == col).astype(F32).astype(BF16)
+        for pos_x, q_ref in ((self.pos_n, qn_ref), (self.pos_f, qf_ref)):
+            order = jnp.broadcast_to(self.own(me, pos_x), (8, t)).astype(BF16)
+            column = dot_nt(eye, order)[:, 0:1]
+            q_ref[...] = (col == column.astype(jnp.int32)).astype(F32).astype(BF16)
+
+
+def route_kernel(slots, sizes, several, expert_ref, slot_ref, gate_ref, every, pick_ref, mine, top, tops, send_sem, recv_sem, top_send, top_recv):
     me = Place()
     t = expert_ref.shape[1]
-    slot = slot_ref[...]
-    mine[0:2] = jnp.where(slot < slots, expert_ref[...], -1).astype(F32)
-    mine[2:4] = jnp.minimum(slot, slots).astype(F32)
-    mine[4:6] = gate_ref[...]
-    mine[6:8] = jnp.zeros((2, t), F32)
-
     barrier = pltpu.get_barrier_semaphore()
     peers = [(me.dp, lax.rem(me.ep + i, 8)) for i in range(1, 8)]
     groups = [(lax.rem(me.dp + i, 4), me.ep) for i in range(1, 4)]
@@ -63,6 +128,11 @@
         groups = []
     for peer in peers + groups:
         pl.semaphore_signal(barrier, inc=1, device_id=peer, device_id_type=MESH)
+    slot = slot_ref[...]
+    mine[0:2] = jnp.where(slot < slots, expert_ref[...], -1).astype(F32)
+    mine[2:4] = jnp.minimum(slot, slots).astype(F32)
+    mine[4:6] = gate_ref[...]
+    mine[6:8] = jnp.zeros((2, t), F32)
     pl.semaphore_wait(barrier, len(peers) + len(groups))
 
     def table_to(i):
@@ -92,36 +162,12 @@
     for i in range(1, 8):
         table_from(i).wait_recv()
 
-    e = [every[:, 0, :], every[:, 1, :]]
-    s = [every[:, 2, :], every[:, 3, :]]
-    g = [every[:, 4, :], every[:, 5, :]]
-    src = lax.broadcasted_iota(jnp.int32, (8, t), 0)
-    lane = lax.broadcasted_iota(jnp.int32, (8, t), 1)
-    zs, cs = src // 2, src % 2
-    near = zs + 1 - 2 * (zs % 2)
-    inner, end = 2 - zs // 2, 3 - 3 * (zs // 2)
-    chip = [jnp.floor(v * 0.25).astype(jnp.int32) for v in e]
-
-    def needs(where):
-        return jnp.logical_or(chip[0] == where, chip[1] == where)
-
-    m_n, m_a = needs(near), needs(end)
-    m_b = jnp.logical_and(needs(inner), jnp.logical_not(m_a))
-    row = lax.broadcasted_iota(jnp.int32, (t, t), 0)
-    col = lax.broadcasted_iota(jnp.int32, (t, t), 1)
-    before = (row < col).astype(F32).astype(BF16)
-
-    def count(mask):
-        return dot(mask.astype(F32).astype(BF16), before).astype(jnp.int32)
-
-    total_a = jnp.sum(m_a.astype(F32), axis=1, keepdims=True).astype(jnp.int32)
-    pos_n = jnp.where(m_n, count(m_n), -1)
-    pos_f = jnp.where(m_a, count(m_a), jnp.where(m_b, total_a + count(m_b), -1))
+    packs = Packs(me, every)
     def most(mask):
         return jnp.max(jnp.sum(mask.astype(F32), axis=1, keepdims=True), axis=0, keepdims=True)
 
-    far_top = most(jnp.logical_or(m_a, m_b))
-    end_top = jnp.maximum(most(m_a), most(m_n))
+    far_top = most(jnp.logical_or(packs.m_a, packs.m_b))
+    end_top = jnp.maximum(most(packs.m_a), most(packs.m_n))
     which = lax.broadcasted_iota(jnp.int32, (8, 128), 0)
     top[...] = jnp.where(which == 0, far_top, end_top)
 
@@ -138,39 +184,6 @@
     for i in range(len(groups)):
         top_copy(i, i).start()
 
-    pos = jnp.where(zs == me.z, lane, jnp.where(zs == me.near, pos_n, pos_f))
-
-    codes = []
-    for j in range(2):
-        local = e[j].astype(jnp.int32) - 2 * me.ep
-        hit = jnp.logical_and(local >= 0, local < 2)
-        code = local * (2 * slots) + cs * slots + s[j].astype(jnp.int32) + 1
-        codes.append(jnp.where(hit, code, 0).astype(F32))
-    table = jnp.concatenate(codes + g, axis=0).astype(BF16)
-    slot_row = lax.broadcasted_iota(jnp.int32, (4 * slots, t), 0) + 1
-    slot_col = lax.broadcasted_iota(jnp.int32, (t, 4 * slots), 1) + 1
-    for k in range(8):
-        perm = (row == pos[k : k + 1]).astype(F32).astype(BF16)
-        by_row = dot_nt(table, perm)
-        by_col = dot_nt(perm, table)
-        r0 = by_row[k : k + 1].astype(jnp.int32)
-        r1 = by_row[8 + k : 9 + k].astype(jnp.int32)
-        c0 = by_col[:, k : k + 1].astype(jnp.int32)
-        c1 = by_col[:, 8 + k : 9 + k].astype(jnp.int32)
-        g0, g1 = by_col[:, 16 + k : 17 + k], by_col[:, 24 + k : 25 + k]
-        hit = jnp.logical_or(slot_row == r0, slot_row == r1)
-        place = slice((k % 2) * t, (k % 2 + 1) * t)
-        a_ref[k // 2, :, place] = hit.astype(F32).astype(BF16)
-        weight = jnp.where(slot_col == c0, g0, 0.0) + jnp.where(slot_col == c1, g1, 0.0)
-        cw_ref[k // 2, place, :] = weight.astype(BF16)
-
-    eye = (row == col).astype(F32).astype(BF16)
-    for pos_x, p_ref, q_ref in ((pos_n, pn_ref, qn_ref), (pos_f, pf_ref, qf_ref)):
-        order = jnp.sum(jnp.where(src == me.ep, pos_x, 0).astype(F32), axis=0, keepdims=True)
-        p_ref[...] = (row == order.astype(jnp.int32)).astype(F32).astype(BF16)
-        column = dot_nt(eye, jnp.broadcast_to(order, (8, t)).astype(BF16))[:, 0:1]
-        q_ref[...] = (col == column.astype(jnp.int32)).astype(F32).astype(BF16)
-
     limit = top[...]
     for i in range(len(groups)):
         top_copy(i, i).wait_recv()
@@ -179,14 +192,14 @@
     pick = jnp.full((1, 128), len(sizes) - 1, jnp.int32)
     for i, (far_rows, end_rows) in reversed(list(enumerate(sizes[:-1]))):
         pick = jnp.where(jnp.logical_and(far_max <= far_rows, end_max <= end_rows), i, pick)
-    pick_ref[...] = jnp.broadcast_to(pick, (8, 128))
+    pick_ref[0, 0] = jnp.max(pick)
     for i in range(7):
         table_to(i).wait_send()
     for i in range(len(groups)):
         top_copy(i, i).wait_send()
 
 
-def up_kernel(far_rows, end_rows, x_ref, a_ref, pn_ref, pf_ref, wg_hbm, wu_hbm, h_ref, xall, sn, sf, zbuf, gacc, uacc, wgb, wub, wsem, send_sem, recv_sem):
+def up_kernel(unroll, slots, far_rows, end_rows, x_ref, every, a_ref, cw_ref, pn_ref, pf_ref, qn_ref, qf_ref, wg_hbm, wu_hbm, h_ref, xall, sn, sf, zbuf, gacc, uacc, wgb, wub, wsem, send_sem, recv_sem):
     me = Place()
     t, d = x_ref.shape
     ff = wg_hbm.shape[2]
@@ -206,16 +219,11 @@
                 wsem.at[p, i],
             )
 
-    for p in range(parts - 1):
+    barrier = pltpu.get_barrier_semaphore()
+    me.greet(barrier)
+    for p in range(parts):
         for copy in weights(0, p):
             copy.start()
-
-    def clear(j, _):
-        xall[j] = jnp.zeros(xall.shape[1:], BF16)
-        return 0
-
-    lax.fori_loop(0, n, clear, 0)
-    me.barrier()
 
     def cell(j, slot, count):
         return xall.at[j, pl.ds(pl.multiple_of(slot * t, t), count)]
@@ -252,11 +260,40 @@
         sf[j] = dot(pf_ref[:far_rows], block).astype(BF16)
         sn[j] = dot(pn_ref[:end_rows], block).astype(BF16)
         xall[j, pl.ds(pl.multiple_of(own * t, t), t)] = block
+        return 0
+
+    def send(j):
         for copy in sends(j):
             copy.start()
+
+    def clear(j, _):
+        def zero(slot, start, stop):
+            if stop > start:
+                xall[j, pl.ds(pl.multiple_of(slot * t + start, 16), stop - start)] = jnp.zeros((stop - start, CW), BF16)
+
+        for i in range(2):
+            zero(2 * me.near + i, end_rows, t)
+            for f in me.far:
+                zero(2 * f + i, far_rows, t)
+
+        @pl.when(me.end)
+        def _():
+            for i in range(2):
+                for f in me.far:
+                    zero(2 * f + i, end_rows, far_rows)
+
         return 0
 
-    lax.fori_loop(0, AHEAD, pack, 0)
+    packs = Packs(me, every)
+    packs.order(me)
+    packs.packers(me, pn_ref, pf_ref)
+    for j in range(AHEAD):
+        pack(j, 0)
+        if j == 0:
+            pl.semaphore_wait(barrier, 7)
+        send(j)
+    lax.fori_loop(AHEAD, n, pack, 0)
+    lax.fori_loop(0, n, clear, 0)
 
     def clear_sums(i, _):
         cols = pl.ds(pl.multiple_of(i * CW, CW), CW)
@@ -296,21 +333,13 @@
             gather(k)
 
         def tiles_of(p, last):
-            for copy in weights(u, p):
-                copy.wait()
-            later, q = (u, p + parts - 1) if p == 0 else (u + 1, p - 1)
-
-            def start():
-                for copy in weights(later, q):
-                    copy.start()
-
-            if p > 0 and last:
-                pl.when(later < 2 * nk)(start)
-            else:
-                start()
-            for i in range(sizes[p]):
-                here = pl.ds(i * CW, CW)
-                cols = pl.ds((starts[p] + i) * CW, CW)
+            if p % 2 == 0:
+                for r in range(p, min(parts, p + 2)):
+                    for copy in weights(u, r):
+                        copy.wait()
+            def tile(i, _):
+                here = pl.ds(pl.multiple_of(i * CW, CW), CW)
+                cols = pl.ds(pl.multiple_of((starts[p] + i) * CW, CW), CW)
                 z = zbuf[e]
                 gate = gacc[e, :, cols] + dot(z, wgb[p, :, here])
                 up = uacc[e, :, cols] + dot(z, wub[p, :, here])
@@ -319,6 +348,18 @@
                 else:
                     gacc[e, :, cols] = gate
                     uacc[e, :, cols] = up
+                return 0
+
+            lax.fori_loop(0, sizes[p], tile, 0, unroll=unroll)
+
+            def start():
+                for copy in weights(u + 1, p):
+                    copy.start()
+
+            if last:
+                pl.when(u + 1 < 2 * nk)(start)
+            else:
+                start()
 
         @pl.when(k < nk - 1)
         def _():
@@ -330,10 +371,10 @@
             for p in range(parts):
                 tiles_of(p, True)
 
-    def step(j, _):
+    def relay(j):
         @pl.when(j + AHEAD < n)
         def _():
-            pack(j + AHEAD, 0)
+            send(j + AHEAD)
 
         @pl.when(j < n)
         def _():
@@ -353,13 +394,18 @@
                 arrived(j - 1, slot, end_rows)
                 forward(j - 1, 4 + i, slot, end_rows, partner).start()
 
+    def step(j, _):
+        relay(j)
+
         @pl.when(j >= 3)
         def _():
             unit(j - 3)
 
         return 0
 
-    lax.fori_loop(0, n + 3, step, 0)
+    relay(jnp.int32(0))
+    packs.matrices(me, slots, a_ref, cw_ref, qn_ref, qf_ref)
+    lax.fori_loop(1, n + 3, step, 0)
 
     def drain(j, _):
         for copy in sends(j):
@@ -382,7 +428,7 @@
     lax.fori_loop(0, n, drain, 0)
 
 
-def down_kernel(far_rows, end_rows, h_ref, cw_ref, qn_ref, qf_ref, wd_hbm, y_ref, o, yd, yn, yf, yr, sd, sn, sf, wdb, wsem, send_sem, dsem, nsem, fsem, rsem):
+def down_kernel(far_rows, end_rows, h_ref, cw_ref, qn_ref, qf_ref, wd_hbm, y_hbm, y_ref, y_sem, o, yd, yn, yf, yr, sd, sn, sf, wdb, wsem, send_sem, dsem, nsem, fsem, rsem, ready):
     me = Place()
     t, d = y_ref.shape
     ff = wd_hbm.shape[1]
@@ -398,10 +444,10 @@
         for e in range(2):
             yield pltpu.make_async_copy(wd_hbm.at[e, :, cols], wdb.at[slot, e], wsem.at[slot, e])
 
+    me.greet(ready)
     for q in range(depth - 1):
         for copy in weights(q):
             copy.start()
-    me.barrier()
 
     partner, nearby = me.dev(me.z, 1 - me.c), me.dev(me.near, me.c)
 
@@ -421,6 +467,10 @@
 
     def to_far(q, i):
         return remote(q, 2 + i, sf.at[q, i], yf.at[q], fsem.at[q], me.dev(me.far[i], me.c))
+
+    def result(q):
+        cols = pl.ds(pl.multiple_of(q * CW, CW), CW)
+        return pltpu.make_async_copy(y_ref.at[:, cols], y_hbm.at[:, cols], y_sem.at[q])
 
     def part(q, zs, c, count):
         return dot(cw_ref[zs, pl.ds(pl.multiple_of(c * t, t), count), :], o[q, zs])
@@ -447,6 +497,11 @@
                     o[q, zs, e * size : (e + 1) * size] = block[zs * size : (zs + 1) * size]
             for zs in range(4):
                 sd[q, zs * t : (zs + 1) * t] = part(q, zs, 1 - me.c, t).astype(BF16)
+
+            @pl.when(q == 0)
+            def _():
+                pl.semaphore_wait(ready, 7)
+
             to_partner(q).start()
 
         @pl.when(jnp.logical_and(q >= 1, q <= n))
@@ -483,12 +538,14 @@
             total += dot(qn_ref[:, :end_rows], yn[r])
             total += dot(qf_ref[:, :far_rows], yf[r])
             y_ref[:, pl.ds(pl.multiple_of(r * CW, CW), CW)] = total.astype(BF16)
+            result(r).start()
 
         return 0
 
     lax.fori_loop(0, n + lag, step, 0)
 
     def drain(q, _):
+        result(q).wait()
         to_partner(q).wait_send()
         to_near(q).wait_send()
 
@@ -507,89 +564,91 @@
     lax.fori_loop(0, n, drain, 0)
 
 
-def up_call(x, a, pn, pf, w_gate, w_up, slots, far_rows, end_rows, ident):
+def moe_kernel(unroll, slots, far_rows, end_rows, x, every, wg, wu, wd, y, h, a, cw, pn, pf, qn, qf, ready, up_wsem, up_send, up_recv, down_wsem, down_send, dsem, nsem, fsem, rsem, y_sem):
+    t, d = x.shape
+    n, rows, ff = d // CW, h.shape[1], h.shape[2]
+    parts = up_wsem.shape[0]
+    wide = -(-(ff // CW) // parts) * CW
+
+    def first(xall, sn, sf, zbuf, gacc, uacc, wgb, wub):
+        up_kernel(unroll, slots, far_rows, end_rows, x, every, a, cw, pn, pf, qn, qf, wg, wu, h, xall, sn, sf, zbuf, gacc, uacc, wgb, wub, up_wsem, up_send, up_recv)
+
+    pl.run_scoped(
+        first,
+        pltpu.VMEM((n, 8 * t, CW), BF16),
+        pltpu.VMEM((n, end_rows, CW), BF16),
+        pltpu.VMEM((n, far_rows, CW), BF16),
+        pltpu.VMEM((2, rows, KC), BF16),
+        pltpu.VMEM((2, rows, ff), F32),
+        pltpu.VMEM((2, rows, ff), F32),
+        pltpu.VMEM((parts, KC, wide), BF16),
+        pltpu.VMEM((parts, KC, wide), BF16),
+    )
+
+    def second(y_stage, o, yd, yn, yf, yr, sd, sn, sf, wdb):
+        down_kernel(far_rows, end_rows, h, cw, qn, qf, wd, y, y_stage, y_sem, o, yd, yn, yf, yr, sd, sn, sf, wdb, down_wsem, down_send, dsem, nsem, fsem, rsem, ready)
+
+    pl.run_scoped(
+        second,
+        pltpu.VMEM((t, d), BF16),
+        pltpu.VMEM((n, 4, rows // 2, CW), BF16),
+        pltpu.VMEM((n, 4 * t, CW), BF16),
+        pltpu.VMEM((n, end_rows, CW), BF16),
+        pltpu.VMEM((n, far_rows, CW), BF16),
+        pltpu.VMEM((n, 2, end_rows, CW), BF16),
+        pltpu.VMEM((n, 4 * t, CW), BF16),
+        pltpu.VMEM((n, end_rows, CW), BF16),
+        pltpu.VMEM((n, 2, far_rows, CW), BF16),
+        pltpu.VMEM((down_wsem.shape[0], 2, ff, CW), BF16),
+    )
+
+
+def moe_call(x, every, w_gate, w_up, w_down, slots, far_rows, end_rows, unroll, ident):
     t, d = x.shape
     ff = w_gate.shape[2]
     n, rows = d // CW, 8 * slots
-    tiles = ff // CW
-    parts = min(4, tiles)
-    wide = -(-tiles // parts) * CW
+    parts = min(4, ff // CW)
     vmem, hbm = pl.BlockSpec(memory_space=pltpu.VMEM), pl.BlockSpec(memory_space=pl.ANY)
     return pl.pallas_call(
-        functools.partial(up_kernel, far_rows, end_rows),
-        out_shape=jax.ShapeDtypeStruct((2, rows, ff), BF16),
-        in_specs=[vmem] * 4 + [hbm] * 2,
-        out_specs=vmem,
+        functools.partial(moe_kernel, unroll, slots, far_rows, end_rows),
+        out_shape=jax.ShapeDtypeStruct((t, d), BF16),
+        in_specs=[vmem] * 2 + [hbm] * 3,
+        out_specs=hbm,
         scratch_shapes=[
-            pltpu.VMEM((n, 8 * t, CW), BF16),
-            pltpu.VMEM((n, end_rows, CW), BF16),
-            pltpu.VMEM((n, far_rows, CW), BF16),
-            pltpu.VMEM((2, rows, KC), BF16),
-            pltpu.VMEM((2, rows, ff), F32),
-            pltpu.VMEM((2, rows, ff), F32),
-            pltpu.VMEM((parts, KC, wide), BF16),
-            pltpu.VMEM((parts, KC, wide), BF16),
+            pltpu.VMEM((2, rows, ff), BF16),
+            pltpu.VMEM((4, 4 * slots, 2 * t), BF16),
+            pltpu.VMEM((4, 2 * t, 4 * slots), BF16),
+            pltpu.VMEM((t, t), BF16),
+            pltpu.VMEM((t, t), BF16),
+            pltpu.VMEM((t, t), BF16),
+            pltpu.VMEM((t, t), BF16),
+            pltpu.SemaphoreType.REGULAR,
             pltpu.SemaphoreType.DMA((parts, 2)),
             pltpu.SemaphoreType.DMA((n, 8)),
             pltpu.SemaphoreType.DMA((n, 8)),
-        ],
-        compiler_params=pltpu.CompilerParams(collective_id=ident, has_side_effects=True, vmem_limit_bytes=VMEM_BYTES),
-        name=f"up_{far_rows}_{end_rows}",
-    )(x, a, pn, pf, w_gate, w_up)
-
-
-def down_call(h, cw, qn, qf, w_down, far_rows, end_rows, ident):
-    _, rows, ff = h.shape
-    d, t = w_down.shape[2], qn.shape[0]
-    n = d // CW
-    vmem, hbm = pl.BlockSpec(memory_space=pltpu.VMEM), pl.BlockSpec(memory_space=pl.ANY)
-    return pl.pallas_call(
-        functools.partial(down_kernel, far_rows, end_rows),
-        out_shape=jax.ShapeDtypeStruct((t, d), BF16),
-        in_specs=[vmem] * 4 + [hbm],
-        out_specs=vmem,
-        scratch_shapes=[
-            pltpu.VMEM((n, 4, rows // 2, CW), BF16),
-            pltpu.VMEM((n, 4 * t, CW), BF16),
-            pltpu.VMEM((n, end_rows, CW), BF16),
-            pltpu.VMEM((n, far_rows, CW), BF16),
-            pltpu.VMEM((n, 2, end_rows, CW), BF16),
-            pltpu.VMEM((n, 4 * t, CW), BF16),
-            pltpu.VMEM((n, end_rows, CW), BF16),
-            pltpu.VMEM((n, 2, far_rows, CW), BF16),
-            pltpu.VMEM((3, 2, ff, CW), BF16),
             pltpu.SemaphoreType.DMA((3, 2)),
             pltpu.SemaphoreType.DMA((n, 4)),
             pltpu.SemaphoreType.DMA((n,)),
             pltpu.SemaphoreType.DMA((n,)),
             pltpu.SemaphoreType.DMA((n,)),
             pltpu.SemaphoreType.DMA((n, 2)),
+            pltpu.SemaphoreType.DMA((n,)),
         ],
         compiler_params=pltpu.CompilerParams(collective_id=ident, has_side_effects=True, vmem_limit_bytes=VMEM_BYTES),
-        name=f"down_{far_rows}_{end_rows}",
-    )(h, cw, qn, qf, w_down)
+        name=f"moe_{far_rows}_{end_rows}",
+    )(x, every, w_gate, w_up, w_down)
 
 
 def route_call(expert, slot, gate, slots, sizes, several):
     t = expert.shape[1]
     vmem = pl.BlockSpec(memory_space=pltpu.VMEM)
-    square = jax.ShapeDtypeStruct((t, t), BF16)
     return pl.pallas_call(
         functools.partial(route_kernel, slots, sizes, several),
-        out_shape=[
-            jax.ShapeDtypeStruct((4, 4 * slots, 2 * t), BF16),
-            jax.ShapeDtypeStruct((4, 2 * t, 4 * slots), BF16),
-            square,
-            square,
-            square,
-            square,
-            jax.ShapeDtypeStruct((8, 128), jnp.int32),
-        ],
+        out_shape=[jax.ShapeDtypeStruct((8, 8, t), F32), jax.ShapeDtypeStruct((1, 1), jnp.int32)],
         in_specs=[vmem] * 3,
-        out_specs=[vmem] * 7,
+        out_specs=[vmem, pl.BlockSpec(memory_space=pltpu.SMEM)],
         scratch_shapes=[
             pltpu.VMEM((8, t), F32),
-            pltpu.VMEM((8, 8, t), F32),
             pltpu.VMEM((8, 128), F32),
             pltpu.VMEM((3, 8, 128), F32),
             pltpu.SemaphoreType.DMA((7,)),
@@ -608,13 +667,12 @@
         t = x.shape[0]
         slots = 5 * t * 2 // (4 * 16)
         sizes = [(160, 112), (192, 144), (t, 4 * slots)]
-        a, cw, pn, pf, qn, qf, pick = route_call(expert.T, slot.T, gate.T, slots, sizes, mesh.shape["dp"] > 1)
+        every, pick = route_call(expert.T, slot.T, gate.T, slots, sizes, mesh.shape["dp"] > 1)
 
         def branch(i):
             def run(x, w_gate, w_up, w_down):
                 far_rows, end_rows = sizes[i]
-                h = up_call(x, a, pn, pf, w_gate, w_up, slots, far_rows, end_rows, 1 + 2 * i)
-                return down_call(h, cw, qn, qf, w_down, far_rows, end_rows, 2 + 2 * i)
+                return moe_call(x, every, w_gate, w_up, w_down, slots, far_rows, end_rows, i == 0, 1 + i)
 
             return run
 

time: 182 us -> 172 us (0.945)
  Pallas kernels: 177 us -> 168 us
    pallas_call x2 -> x1, Pallas kernels: 163 us -> 154 us  [moe_call(): pl.pallas_call(functools.partial(moe_kernel, unroll, slots, far_rows, end...]
where the time goes in v3:
time: 172 us
  Pallas kernels  168 us (98%)
  local copies, waits for them, and re-layouts  2.85 us (2%)
    pallas_call x1, Pallas kernels, moe_call(): pl.pallas_call(functools.partial(moe_kernel, unroll, slots, far_rows, end...  154 us
    pallas_call x1, Pallas kernels, route_call(): pl.pallas_call(functools.partial(route_kernel, slots, sizes, several), ou...  13.9 us

profile of v3, /device:TPU:0, one launch (start us, length us, event | category | flops | bytes accessed | tf_op | source)
XLA Modules:
  0.0 171.6 jit_solution(16496903982000944692)
XLA Ops:
  0.0 13.9 %route.1 = (f32[8,8,256]{2,1,0:T(8,128)}, s32[1,1]{1,0:T(1,128)}) custom-call(s32[2,256]{1,0:T(2,128)} %bitcast.20, s32[2,256]{1,0:T(2,128)} %bitcast.21, f32[2,256]{1,0:T(2,128)} %bitcast.22), custom_call_target="tpu_custom_call" | custom-call | tf_op jit(solution)/shard_map/route/pallas_call | solution.py:645
  14.5 154.2 %conditional.1 = (bf16[1,1,256,3584]{3,2,1,0:T(8,128)(2,1)}) conditional(s32[]{:T(128)} %bitcast.9, (bf16[256,3584]{1,0:T(8,128)(2,1)}, f32[8,8,256]{2,1,0:T(8,128)}, bf16[2,3584,4864]{2,1,0:T(8,128)(2,1)}, bf16[2,3584,4864]{2,1,0:T(8,128)(2,1)}, bf16[2,4864,3584]{2,1,0:T(8,128)(2,1)}) %tuple.24, (bf16[256,3584]{1,0:T(8,128)(2,1)}, ...), branch_computations={%region_0.0_spmd, %region_1.0_spmd, %region_2.0_spmd} | conditional | bytes 8 | solution.py:679
  14.6 154.0 %moe_160_112.1 = bf16[256,3584]{1,0:T(8,128)(2,1)} custom-call(bf16[256,3584]{1,0:T(8,128)(2,1)} %get-tuple-element.40.x, f32[8,8,256]{2,1,0:T(8,128)} %get-tuple-element.41.every, bf16[2,3584,4864]{2,1,0:T(8,128)(2,1)} %get-tuple-element.42.wg, bf16[2,3584,4864]{2,1,0:T(8,128)(2,1)} %get-tuple-element.43.wu, bf16[2,4864,3584]{2,1,0:T(8,128)(2,1)} %get-tuple-element.44.wd), custom_call_target="tpu_custom_call" | custom-call | tf_op jit(solution)/shard_map/cond/branch_0_fun/moe_160_112/pallas_call | solution.py:612
  168.7 2.8 %copy.15 = bf16[1,1,256,3584]{3,2,1,0:T(8,128)(2,1)} copy(bf16[1,1,256,3584]{3,2,1,0:T(8,128)(2,1)} %get-tuple-element.59) | data formatting | bytes 3670016

commit v4 on v3

--- a/solution.py
+++ b/solution.py
@@ -480,44 +480,6 @@
         return part(q, zs, me.c, count) + other
 
     def step(q, _):
-        @pl.when(q < n)
-        def _():
-            for copy in weights(q):
-                copy.wait()
-
-            @pl.when(q + depth - 1 < n)
-            def _():
-                for copy in weights(q + depth - 1):
-                    copy.start()
-
-            slot = lax.rem(q, depth)
-            for e in range(2):
-                block = dot(h_ref[e], wdb[slot, e]).astype(BF16)
-                for zs in range(4):
-                    o[q, zs, e * size : (e + 1) * size] = block[zs * size : (zs + 1) * size]
-            for zs in range(4):
-                sd[q, zs * t : (zs + 1) * t] = part(q, zs, 1 - me.c, t).astype(BF16)
-
-            @pl.when(q == 0)
-            def _():
-                pl.semaphore_wait(ready, 7)
-
-            to_partner(q).start()
-
-        @pl.when(jnp.logical_and(q >= 1, q <= n))
-        def _():
-            r = q - 1
-            to_partner(r).wait_recv()
-
-            @pl.when(me.end)
-            def _():
-                for i, f in enumerate(me.far):
-                    sf[r, i, 0:end_rows] = both(r, f, end_rows).astype(BF16)
-                    relay(r, i).start()
-
-            sn[r] = both(r, me.near, end_rows).astype(BF16)
-            to_near(r).start()
-
         @pl.when(jnp.logical_and(me.inner, jnp.logical_and(q >= 2, q <= n + 1)))
         def _():
             r = q - 2
@@ -528,6 +490,44 @@
                 if far_rows > end_rows:
                     sf[r, i, end_rows:far_rows] = total[end_rows:].astype(BF16)
                 to_far(r, i).start()
+
+        @pl.when(q < n)
+        def _():
+            for copy in weights(q):
+                copy.wait()
+
+            @pl.when(q + depth - 1 < n)
+            def _():
+                for copy in weights(q + depth - 1):
+                    copy.start()
+
+            slot = lax.rem(q, depth)
+            for e in range(2):
+                block = dot(h_ref[e], wdb[slot, e]).astype(BF16)
+                for zs in range(4):
+                    o[q, zs, e * size : (e + 1) * size] = block[zs * size : (zs + 1) * size]
+            for zs in range(4):
+                sd[q, zs * t : (zs + 1) * t] = part(q, zs, 1 - me.c, t).astype(BF16)
+
+            @pl.when(q == 0)
+            def _():
+                pl.semaphore_wait(ready, 7)
+
+            to_partner(q).start()
+
+        @pl.when(jnp.logical_and(q >= 1, q <= n))
+        def _():
+            r = q - 1
+            to_partner(r).wait_recv()
+
+            @pl.when(me.end)
+            def _():
+                for i, f in enumerate(me.far):
+                    sf[r, i, 0:end_rows] = both(r, f, end_rows).astype(BF16)
+                    relay(r, i).start()
+
+            sn[r] = both(r, me.near, end_rows).astype(BF16)
+            to_near(r).start()
 
         @pl.when(q >= lag)
         def _():

time: 172 us -> 172 us (level)
  no operation moved by 1% of the time
where the time goes in v4:
time: 172 us
  Pallas kernels  168 us (98%)
  local copies, waits for them, and re-layouts  2.85 us (2%)
    pallas_call x1, Pallas kernels, moe_call(): pl.pallas_call(functools.partial(moe_kernel, unroll, slots, far_rows, end...  154 us
    pallas_call x1, Pallas kernels, route_call(): pl.pallas_call(functools.partial(route_kernel, slots, sizes, several), ou...  13.9 us

profile of v4, /device:TPU:0, one launch (start us, length us, event | category | flops | bytes accessed | tf_op | source)
XLA Modules:
  0.0 171.6 jit_solution(11680693813684098943)
XLA Ops:
  0.0 13.9 %route.1 = (f32[8,8,256]{2,1,0:T(8,128)}, s32[1,1]{1,0:T(1,128)}) custom-call(s32[2,256]{1,0:T(2,128)} %bitcast.20, s32[2,256]{1,0:T(2,128)} %bitcast.21, f32[2,256]{1,0:T(2,128)} %bitcast.22), custom_call_target="tpu_custom_call" | custom-call | tf_op jit(solution)/shard_map/route/pallas_call | solution.py:645
  14.5 154.2 %conditional.1 = (bf16[1,1,256,3584]{3,2,1,0:T(8,128)(2,1)}) conditional(s32[]{:T(128)} %bitcast.9, (bf16[256,3584]{1,0:T(8,128)(2,1)}, f32[8,8,256]{2,1,0:T(8,128)}, bf16[2,3584,4864]{2,1,0:T(8,128)(2,1)}, bf16[2,3584,4864]{2,1,0:T(8,128)(2,1)}, bf16[2,4864,3584]{2,1,0:T(8,128)(2,1)}) %tuple.24, (bf16[256,3584]{1,0:T(8,128)(2,1)}, ...), branch_computations={%region_0.0_spmd, %region_1.0_spmd, %region_2.0_spmd} | conditional | bytes 8 | solution.py:679
  14.6 154.0 %moe_160_112.1 = bf16[256,3584]{1,0:T(8,128)(2,1)} custom-call(bf16[256,3584]{1,0:T(8,128)(2,1)} %get-tuple-element.40.x, f32[8,8,256]{2,1,0:T(8,128)} %get-tuple-element.41.every, bf16[2,3584,4864]{2,1,0:T(8,128)(2,1)} %get-tuple-element.42.wg, bf16[2,3584,4864]{2,1,0:T(8,128)(2,1)} %get-tuple-element.43.wu, bf16[2,4864,3584]{2,1,0:T(8,128)(2,1)} %get-tuple-element.44.wd), custom_call_target="tpu_custom_call" | custom-call | tf_op jit(solution)/shard_map/cond/branch_0_fun/moe_160_112/pallas_call | solution.py:612
  168.7 2.8 %copy.15 = bf16[1,1,256,3584]{3,2,1,0:T(8,128)(2,1)} copy(bf16[1,1,256,3584]{3,2,1,0:T(8,128)(2,1)} %get-tuple-element.59) | data formatting | bytes 3670016
